TPU v7x, 32 devices: a whole 2x2x4 slice. The times are simulated.
32 devices in a mesh: ens: 4 (over y, x), lon: 8 (over z, core).
Axes of the slice: x: 2, y: 2, z: 4, core: 2. Of those that a mesh axis runs over, the one named last changes fastest.
Arguments:
- control: float32 [8, 1024, 512], P('ens', None, 'lon'), may hold values from -6 to 6
- residual: float32 [8, 1024, 512], P('ens', None, 'lon'), may hold values from -6 to 6
- direction: float32 [8, 1024, 512], P('ens', None, 'lon'), may hold values from -6 to 6
- ens_perturb: bfloat16 [8, 3, 1024, 512], P('ens', None, None, 'lon'), may hold values from -1.5 to 1.5
- localize: float32 [1024, 1024], replicated, may hold values from -0.5 to 1.5
- obs_cell: int32 [32768], P('lon'), may hold values from 0 to 65535
- obs_slot: int32 [32768], P('lon'), may hold values from 0 to 3
- obs_weight: float32 [32768], P('lon'), may hold values from 0.5 to 4
Outputs:
- control_new: float32 [8, 1024, 512], P('ens', None, 'lon')
- residual_new: float32 [8, 1024, 512], P('ens', None, 'lon')
- direction_new: float32 [8, 1024, 512], P('ens', None, 'lon')
Inputs may be any that keep to these rules, and one draw needn't show every extreme that they name: `obs_cell`: row-major cell within the entry's own longitude tile: row times 64 plus column. `obs_slot`: slot n < 3 observes the height after model step n + 1; slot 3 marks a padding entry that observes nothing.
All inputs are finite; a program needn't handle non-finite values.
Results may differ from a plain program's by a relative error of at most 0.0003.
Values sent between devices are 32-bit elements; how exact they have to be, the bound alone decides.
A program may use at most 64 MiB of HBM per device.

v0:
```python
import jax
import jax.numpy as jnp
from jax import lax
from jax.sharding import PartitionSpec as P

STEPS = 3
wave_speed = 0.35
rotation = 0.2


def extended(block, sides, width):
    for axis, dim in sides:
        count = lax.axis_size(axis)
        forward = [(i, i + 1) for i in range(count - 1)]
        forward.append((count - 1, 0))
        backward = [(target, source) for source, target in forward]
        low = lax.ppermute(
            lax.slice_in_dim(block, block.shape[dim] - width, None, axis=dim), axis, forward
        )
        high = lax.ppermute(lax.slice_in_dim(block, 0, width, axis=dim), axis, backward)
        block = jnp.concatenate([low, block, high], axis=dim)
    return block


def grid_factors(row_ids, lat_total):
    latitude = (-1.0 / 3.0 + 2.0 / 3.0 * (row_ids + 0.5) / lat_total) * jnp.pi
    return (1.0 / jnp.cos(latitude), jnp.sin(latitude))


def model_step(fields, orient, metric, coriolis):
    lon_wide = extended(fields, (("lon", 2),), 1)
    lat_wide = jnp.pad(fields, ((0, 0), (1, 1), (0, 0)))
    lon_diff = 0.5 * metric[:, None] * (lon_wide[:, :, 2:] - lon_wide[:, :, :-2])
    lat_diff = 0.5 * (lat_wide[:, 2:] - lat_wide[:, :-2])
    height, zonal, meridional = (fields[0], fields[1], fields[2])
    speed = orient * wave_speed
    turning = orient * rotation * coriolis[:, None]
    return jnp.stack(
        [
            height - speed * (lon_diff[1] + lat_diff[2]),
            zonal - speed * lon_diff[0] + turning * meridional,
            meridional - speed * lat_diff[0] - turning * zonal,
        ]
    )


def body(control, residual, direction, ens_perturb, localize, obs_cell, obs_slot, obs_weight):
    hi = lax.Precision.HIGHEST
    lat_total = localize.shape[0]
    tile_cols = control.shape[2]
    localized = jnp.einsum("ij,mjc->mic", localize, direction, precision=hi)
    increment = jnp.sum(ens_perturb.astype(jnp.float32) * localized[:, None], axis=0)
    lat_slab = lax.psum(increment, "ens")
    slab_rows = lat_slab.shape[1]
    cells = slab_rows * tile_cols
    row_ids = jnp.arange(slab_rows, dtype=jnp.int32).astype(jnp.float32)
    metric, coriolis = grid_factors(row_ids, lat_total)
    local_row = obs_cell // tile_cols
    inside = (local_row >= 0) & (local_row < slab_rows) & (obs_slot < STEPS)
    cell_index = jnp.clip(local_row, 0, slab_rows - 1) * tile_cols + obs_cell % tile_cols
    slot_index = obs_slot * cells + cell_index
    gather_index = jnp.clip(slot_index, 0, STEPS * cells - 1)
    tl_state = lat_slab
    heights = []
    for moment in range(STEPS):
        tl_state = model_step(tl_state, 1.0, metric, coriolis)
        heights.append(tl_state[0].reshape(-1))
    observed = jnp.concatenate(heights)[gather_index]
    weighted = jnp.where(inside, obs_weight * observed, 0.0)
    forcing = jnp.zeros(((STEPS + 1) * cells,), jnp.float32).at[slot_index].add(weighted)
    forcing = forcing.reshape(STEPS + 1, slab_rows, tile_cols)
    adjoint = jnp.zeros(lat_slab.shape, jnp.float32)
    for moment in reversed(range(STEPS)):
        adjoint = adjoint.at[0].add(forcing[moment])
        adjoint = model_step(adjoint, -1.0, metric, coriolis)
    projected = jnp.sum(ens_perturb.astype(jnp.float32) * adjoint[None], axis=1)
    pulled_back = jnp.einsum("ji,mjc->mic", localize, projected, precision=hi)
    image_vec = direction + pulled_back
    norm_old, curvature, cross_term, square = lax.psum(
        (
            jnp.sum(residual * residual),
            jnp.sum(direction * image_vec),
            jnp.sum(residual * image_vec),
            jnp.sum(image_vec * image_vec),
        ),
        ("ens", "lon"),
    )
    step_size = norm_old / curvature
    control_new = control + step_size * direction
    residual_new = residual - step_size * image_vec
    norm_new = norm_old - 2.0 * step_size * cross_term + step_size * step_size * square
    direction_new = residual_new + norm_new / norm_old * direction
    return (control_new, residual_new, direction_new)


def solution(mesh):
    in_specs = (
        P("ens", None, "lon"),
        P("ens", None, "lon"),
        P("ens", None, "lon"),
        P("ens", None, None, "lon"),
        P(),
        P("lon"),
        P("lon"),
        P("lon"),
    )
    out_specs = (P("ens", None, "lon"), P("ens", None, "lon"), P("ens", None, "lon"))
    return jax.shard_map(body, mesh=mesh, in_specs=in_specs, out_specs=out_specs, check_vma=False)
```

profile of v0, /device:TPU:12, one launch (start us, length us, event | category | flops | bytes accessed | tf_op | source)
XLA Modules:
  0.0 210.3 jit_solution(16358781422589472048)
XLA Ops:
  7.2 6.8 %fusion.6 = f32[2,1024,64]{1,2,0:T(8,128)S(1)} fusion(f32[2,1024,64]{1,2,0:T(8,128)} %param.16, f32[1024,1024]{1,0:T(8,128)} %param.18), kind=kOutput, calls=%fused_computation.10 | convolution fusion | flops 1610612736 | bytes 5242880 | tf_op jit(solution)/shard_map/ij,mjc->mic/dot_general | solution.py:51
  14.1 1.1 fusion.4
  15.3 49.7 %all-reduce.10.cloned.1.call-done = f32[3,1024,64]{1,2,0:T(8,128)} async-done(((f32[3,1024,64]{1,2,0:T(8,128)}), f32[3,1024,64]{1,2,0:T(8,128)}) %all-reduce.10.cloned.1.call-update) | async-done | bytes 786448 | tf_op jit(solution)/shard_map/psum | solution.py:53
  65.0 1.0 fusion.89
  67.5 1.8 collective-permute-done.1
  69.2 2.8 %fusion.34 = (f32[3,1024,64]{1,2,0:T(8,128)S(1)}, f32[3,1024,64]{1,2,0:T(8,128)S(1)}) fusion(f32[3,1024,64]{1,2,0:T(8,128)} %all-reduce.10.cloned.1.call-done, f32[3,1024,1]{1,2,0:T(1,128)S(1)} %collective-permute-done.1, f32[3,1024,1]{1,2,0:T(1,128)S(1)} %collective-permute-done, f32[1024]{0:T(1024)S(1)} %divide_multiply_fusion), kind=kLoop, calls=%fused_computation.57 | loop fusion | flops 1179648 | bytes 2387968 | tf_op jit(solution)/shard_map/mul | solution.py:33
  72.0 1.3 fusion.70
  75.6 4.2 %collective-permute-done.3 = f32[3,1024,1]{1,2,0:T(1,128)S(1)} collective-permute-done((f32[3,1024,1]{1,2,0:T(1,128)S(1)}, f32[3,1024,1]{1,2,0:T(1,128)S(1)}, u32[]{:S(2)}, u32[]{:S(2)}) %collective-permute-start.3) | collective-permute-done | bytes 12320 | tf_op jit(solution)/shard_map/ppermute | solution.py:17
  80.0 0.9 fusion.82
  81.6 1.3 pad_slice_fusion.7
  82.9 1.1 copy.13
  84.2 1.8 collective-permute-done.5
  86.1 1.1 fusion.57
  87.6 23.0 %gather_fusion = f32[4096]{0:T(1024)S(1)} fusion(f32[196608]{0:T(1024)S(1)} %pad_maximum_fusion.16, s32[4096]{0:T(1024)S(1)} %get-tuple-element.53), kind=kCustom, calls=%fused_computation | custom fusion | bytes 49152 | tf_op jit(solution)/shard_map/gather | solution.py:68
  110.7 22.2 %scatter_custom_fusion = f32[262144]{0:T(1024)S(1)} fusion(s32[4096]{0:T(1024)S(1)} %compare_select_fusion.1, f32[4096]{0:T(1024)S(1)} %multiply_select_fusion, f32[]{:T(128)} %constant.120.clone.1), kind=kCustom, calls=%fused_computation.71 | custom fusion | flops 4096 | bytes 1048580 | tf_op jit(solution)/shard_map/scatter-add | solution.py:70
  133.3 1.3 collective-permute-start.6
  135.1 0.9 collective-permute-done.6
  136.0 2.3 %collective-permute-done.7 = f32[3,1024,1]{1,2,0:T(1,128)S(1)} collective-permute-done((f32[3,1024,1]{1,2,0:T(1,128)S(1)}, f32[3,1024,1]{1,2,0:T(1,128)S(1)}, u32[]{:S(2)}, u32[]{:S(2)}) %collective-permute-start.7) | collective-permute-done | bytes 12320 | tf_op jit(solution)/shard_map/ppermute | solution.py:17
  140.2 1.0 collective-permute-done.8
  141.2 4.2 %collective-permute-done.9 = f32[3,1024,1]{1,2,0:T(1,128)S(1)} collective-permute-done((f32[3,1024,1]{1,2,0:T(1,128)S(1)}, f32[3,1024,1]{1,2,0:T(1,128)S(1)}, u32[]{:S(2)}, u32[]{:S(2)}) %collective-permute-start.9) | collective-permute-done | bytes 12320 | tf_op jit(solution)/shard_map/ppermute | solution.py:17
  147.8 3.8 %collective-permute-done.11 = f32[3,1024,1]{1,2,0:T(1,128)S(1)} collective-permute-done((f32[3,1024,1]{1,2,0:T(1,128)S(1)}, f32[3,1024,1]{1,2,0:T(1,128)S(1)}, u32[]{:S(2)}, u32[]{:S(2)}) %collective-permute-start.11) | collective-permute-done | bytes 12320 | tf_op jit(solution)/shard_map/ppermute | solution.py:17
  152.6 3.1 %multiply_reduce_fusion = (f32[]{:T(128)}, f32[]{:T(128)}, f32[]{:T(128)}, f32[]{:T(128)}, f32[2,1024,64]{1,2,0:T(8,128)S(1)}) fusion(f32[2,1024,64]{1,2,0:T(8,128)S(1)} %copy-done.3, f32[2,1024,64]{1,2,0:T(8,128)S(1)} %copy-done.1, f32[2,1024,64]{1,2,0:T(8,128)S(1)} %fusion.5, f32[1024,1024]{1,0:T(8,128)S(1)} %copy-done), kind=kOutput, calls=%fused_computation.66 | convolution fusion | flops 1611792384 | bytes 6291472 | tf_op jit(solution)/shard_map/ji,mjc->mic/dot_general | solution.py:77
  155.7 42.6 %all-reduce.7 = (f32[]{:T(128)}, f32[]{:T(128)}, f32[]{:T(128)}, f32[]{:T(128)}) all-reduce(f32[]{:T(128)} %get-tuple-element.41, f32[]{:T(128)} %get-tuple-element.42, f32[]{:T(128)} %get-tuple-element.40, f32[]{:T(128)} %get-tuple-element.39), channel_id=1, replica_groups=mesh['ens'=4,'lon'=8] {'ens','lon'}, use_global_device_ids=true, to_apply=%region_1.0 | all-reduce | flops 4 | bytes 32 | tf_op jit(solution)/shard_map/psum | solution.py:79
  202.2 1.3 multiply_add_fusion
  (76 shorter events, 11.3 us)
Async XLA Ops:
  7.2 6.9 %copy-start.2 = (bf16[2,3,1024,64]{2,3,1,0:T(8,128)(2,1)S(1)}, bf16[2,3,1024,64]{2,3,1,0:T(8,128)(2,1)}, u32[]{:S(2)}) copy-start(bf16[2,3,1024,64]{2,3,1,0:T(8,128)(2,1)} %param.17) | copy-start | bytes 2359300
  7.2 8.1 %copy-start.5 = (s32[4096]{0:T(1024)S(1)}, s32[4096]{0:T(1024)}, u32[]{:S(2)}) copy-start(s32[4096]{0:T(1024)} %param.19) | copy-start | bytes 49156
  7.2 8.1 %copy-start.6 = (s32[4096]{0:T(1024)S(1)}, s32[4096]{0:T(1024)}, u32[]{:S(2)}) copy-start(s32[4096]{0:T(1024)} %param.20) | copy-start | bytes 49156
  7.2 57.8 %all-reduce.10.cloned.1.call-start = ((), (), s32[]{:S(2)}) async-start(), calls=%async_computation | async-start | bytes 1572864 | tf_op jit(solution)/shard_map/psum | solution.py:53
  66.0 1.5 collective-permute-start
  66.1 3.2 %collective-permute-start.1 = (f32[3,1024,1]{1,2,0:T(1,128)S(1)}, f32[3,1024,1]{1,2,0:T(1,128)S(1)}, u32[]{:S(2)}, u32[]{:S(2)}) collective-permute-start(f32[3,1024,1]{1,2,0:T(1,128)S(1)} %get-tuple-element.95), channel_id=1, source_target_pairs={{0,1},{1,2},{2,3},{3,4},{4,5},{5,6},{6,7},{7,0},{8,9},{9,10},{10,1... | collective-permute-start | bytes 36872 | tf_op jit(solution)/shard_map/ppermute | solution.py:17
  73.4 2.2 %collective-permute-start.2 = (f32[3,1024,1]{1,2,0:T(1,128)S(1)}, f32[3,1024,1]{1,2,0:T(1,128)S(1)}, u32[]{:S(2)}, u32[]{:S(2)}) collective-permute-start(f32[3,1024,1]{1,2,0:T(1,128)S(1)} %get-tuple-element.90), channel_id=1, source_target_pairs={{1,0},{2,1},{3,2},{4,3},{5,4},{6,5},{7,6},{0,7},{9,8},{10,9},{11,1... | collective-permute-start | bytes 36872 | tf_op jit(solution)/shard_map/ppermute | solution.py:20
  74.2 5.6 %collective-permute-start.3 = (f32[3,1024,1]{1,2,0:T(1,128)S(1)}, f32[3,1024,1]{1,2,0:T(1,128)S(1)}, u32[]{:S(2)}, u32[]{:S(2)}) collective-permute-start(f32[3,1024,1]{1,2,0:T(1,128)S(1)} %get-tuple-element.91), channel_id=1, source_target_pairs={{0,1},{1,2},{2,3},{3,4},{4,5},{5,6},{6,7},{7,0},{8,9},{9,10},{10,1... | collective-permute-start | bytes 36872 | tf_op jit(solution)/shard_map/ppermute | solution.py:17
  81.0 3.2 %collective-permute-start.4 = (f32[3,1024,1]{1,2,0:T(1,128)S(1)}, f32[3,1024,1]{1,2,0:T(1,128)S(1)}, u32[]{:S(2)}, u32[]{:S(2)}) collective-permute-start(f32[3,1024,1]{1,2,0:T(1,128)S(1)} %get-tuple-element.85), channel_id=1, source_target_pairs={{1,0},{2,1},{3,2},{4,3},{5,4},{6,5},{7,6},{0,7},{9,8},{10,9},{11,1... | collective-permute-start | bytes 36872 | tf_op jit(solution)/shard_map/ppermute | solution.py:20
  81.1 5.0 %collective-permute-start.5 = (f32[3,1024,1]{1,2,0:T(1,128)S(1)}, f32[3,1024,1]{1,2,0:T(1,128)S(1)}, u32[]{:S(2)}, u32[]{:S(2)}) collective-permute-start(f32[3,1024,1]{1,2,0:T(1,128)S(1)} %get-tuple-element.84), channel_id=1, source_target_pairs={{0,1},{1,2},{2,3},{3,4},{4,5},{5,6},{6,7},{7,0},{8,9},{9,10},{10,1... | collective-permute-start | bytes 36872 | tf_op jit(solution)/shard_map/ppermute | solution.py:17
  87.6 23.1 %copy-start.7 = (f32[4096]{0:T(1024)S(1)}, f32[4096]{0:T(1024)}, u32[]{:S(2)}) copy-start(f32[4096]{0:T(1024)} %param.21) | copy-start | bytes 49156
  133.3 2.7 %collective-permute-start.6 = (f32[3,1024,1]{1,2,0:T(1,128)S(1)}, f32[3,1024,1]{1,2,0:T(1,128)S(1)}, u32[]{:S(2)}, u32[]{:S(2)}) collective-permute-start(f32[3,1024,1]{1,2,0:T(1,128)S(1)} %get-tuple-element.97), channel_id=1, source_target_pairs={{1,0},{2,1},{3,2},{4,3},{5,4},{6,5},{7,6},{0,7},{9,8},{10,9},{11,1... | collective-permute-start | bytes 36872 | tf_op jit(solution)/shard_map/ppermute | solution.py:20
  134.6 3.7 %collective-permute-start.7 = (f32[3,1024,1]{1,2,0:T(1,128)S(1)}, f32[3,1024,1]{1,2,0:T(1,128)S(1)}, u32[]{:S(2)}, u32[]{:S(2)}) collective-permute-start(f32[3,1024,1]{1,2,0:T(1,128)S(1)} %get-tuple-element.98), channel_id=1, source_target_pairs={{0,1},{1,2},{2,3},{3,4},{4,5},{5,6},{6,7},{7,0},{8,9},{9,10},{10,1... | collective-permute-start | bytes 36872 | tf_op jit(solution)/shard_map/ppermute | solution.py:17
  139.2 2.0 collective-permute-start.8
  139.8 5.6 %collective-permute-start.9 = (f32[3,1024,1]{1,2,0:T(1,128)S(1)}, f32[3,1024,1]{1,2,0:T(1,128)S(1)}, u32[]{:S(2)}, u32[]{:S(2)}) collective-permute-start(f32[3,1024,1]{1,2,0:T(1,128)S(1)} %get-tuple-element.78), channel_id=1, source_target_pairs={{0,1},{1,2},{2,3},{3,4},{4,5},{5,6},{6,7},{7,0},{8,9},{9,10},{10,1... | collective-permute-start | bytes 36872 | tf_op jit(solution)/shard_map/ppermute | solution.py:17
  146.3 1.5 collective-permute-start.10
  146.4 6.2 %copy-start = (f32[1024,1024]{1,0:T(8,128)S(1)}, f32[1024,1024]{1,0:T(8,128)}, u32[]{:S(2)}) copy-start(f32[1024,1024]{1,0:T(8,128)} %param.18) | copy-start | bytes 12582916
  146.4 6.2 %copy-start.1 = (f32[2,1024,64]{1,2,0:T(8,128)S(1)}, f32[2,1024,64]{1,2,0:T(8,128)}, u32[]{:S(2)}) copy-start(f32[2,1024,64]{1,2,0:T(8,128)} %param.16) | copy-start | bytes 1572868
  146.4 6.2 %copy-start.3 = (f32[2,1024,64]{1,2,0:T(8,128)S(1)}, f32[2,1024,64]{1,2,0:T(8,128)}, u32[]{:S(2)}) copy-start(f32[2,1024,64]{1,2,0:T(8,128)} %param.15) | copy-start | bytes 1572868
  146.4 5.1 %collective-permute-start.11 = (f32[3,1024,1]{1,2,0:T(1,128)S(1)}, f32[3,1024,1]{1,2,0:T(1,128)S(1)}, u32[]{:S(2)}, u32[]{:S(2)}) collective-permute-start(f32[3,1024,1]{1,2,0:T(1,128)S(1)} %get-tuple-element.74), channel_id=1, source_target_pairs={{0,1},{1,2},{2,3},{3,4},{4,5},{5,6},{6,7},{7,0},{8,9},{9,10},{10,1... | collective-permute-start | bytes 36872 | tf_op jit(solution)/shard_map/ppermute | solution.py:17
  152.3 49.9 %copy-start.4 = (f32[2,1024,64]{1,2,0:T(8,128)S(1)}, f32[2,1024,64]{1,2,0:T(8,128)}, u32[]{:S(2)}) copy-start(f32[2,1024,64]{1,2,0:T(8,128)} %param.14) | copy-start | bytes 1572868
Sparse Core Ops, SparseCore 0:
  15.3 49.6 all-reduce.9
where the time goes:
time: 211 us; the launch traced here: 210 us
  waiting for transfers between devices  72.1 us (34%)
  blocking collectives  42.6 us (20%)
  other arithmetic  34.3 us (16%)
  local copies, waits for them, and re-layouts  28.5 us (14%)
  between operations  18.5 us (9%)
  matrix products  9.88 us (5%)
  starting transfers between devices  4.47 us (2%)
    psum x1, waiting for transfers between devices, body(): lat_slab = lax.psum(increment, 'ens')  49.7 us
    psum x1, blocking collectives, body(): lax.psum((jnp.sum(residual * residual), jnp.sum(direction * image_vec), j...  42.6 us
    gather x1, local copies, waits for them, and re-layouts, body(): observed = jnp.concatenate(heights)[gather_index]  23 us
    scatter-add x1, other arithmetic, body(): jnp.zeros(((STEPS + 1) * cells,), jnp.float32).at[slot_index].add(weighted)  22.2 us
    ppermute x6, waiting for transfers between devices, extended(): lax.ppermute(lax.slice_in_dim(block, block.shape[dim] - width, None, axis...  18.1 us
    dot_general x1, matrix products, body(): localized = jnp.einsum('ij,mjc->mic', localize, direction, precision=hi)  6.79 us
    mul x6, other arithmetic, model_step(): 0.5 * metric[:, None] * (lon_wide[:, :, 2:] - lon_wide[:, :, :-2])  4.76 us
    ppermute x6, waiting for transfers between devices, extended(): lax.ppermute(lax.slice_in_dim(block, 0, width, axis=dim), axis, backward)  4.27 us
  transfers between devices with their start and end apart: 13, of which 12 were waited for; matrix products, arithmetic and copies ran while one was open for 2% of the time, Pallas kernels for 0%

commit v1 on v0

--- a/solution.py
+++ b/solution.py
@@ -50,7 +50,7 @@
     tile_cols = control.shape[2]
     localized = jnp.einsum("ij,mjc->mic", localize, direction, precision=hi)
     increment = jnp.sum(ens_perturb.astype(jnp.float32) * localized[:, None], axis=0)
-    lat_slab = lax.psum(increment, "ens")
+    lat_slab = jnp.sum(lax.all_gather(increment, "ens"), axis=0)
     slab_rows = lat_slab.shape[1]
     cells = slab_rows * tile_cols
     row_ids = jnp.arange(slab_rows, dtype=jnp.int32).astype(jnp.float32)

time: 211 us -> 204 us (0.967)
  waiting for transfers between devices: 72.1 us -> 67.4 us
    psum x1 -> x0, waiting for transfers between devices: 49.7 us -> none  [body(): lat_slab = lax.psum(increment, 'ens')]
    all_gather x0 -> x1, waiting for transfers between devices: none -> 45 us  [body(): lat_slab = jnp.sum(lax.all_gather(increment, 'ens'), axis=0)]
    reduce_sum x0 -> x1, other arithmetic: none -> 2.26 us  [body(): lat_slab = jnp.sum(lax.all_gather(increment, 'ens'), axis=0)]
    mul x6, other arithmetic: 4.76 us -> 2.55 us  [model_step(): 0.5 * metric[:, None] * (lon_wide[:, :, 2:] - lon_wide[:, :, :-2])]
where the time goes in v1:
time: 204 us; the launch traced here: 203 us
  waiting for transfers between devices  67.4 us (33%)
  blocking collectives  42.5 us (21%)
  other arithmetic  33.2 us (16%)
  local copies, waits for them, and re-layouts  27.6 us (14%)
  between operations  18.5 us (9%)
  matrix products  9.88 us (5%)
  starting transfers between devices  4.44 us (2%)
    all_gather x1, waiting for transfers between devices, body(): lat_slab = jnp.sum(lax.all_gather(increment, 'ens'), axis=0)  45 us
    psum x1, blocking collectives, body(): lax.psum((jnp.sum(residual * residual), jnp.sum(direction * image_vec), j...  42.5 us
    gather x1, local copies, waits for them, and re-layouts, body(): observed = jnp.concatenate(heights)[gather_index]  23 us
    scatter-add x1, other arithmetic, body(): jnp.zeros(((STEPS + 1) * cells,), jnp.float32).at[slot_index].add(weighted)  22.2 us
    ppermute x6, waiting for transfers between devices, extended(): lax.ppermute(lax.slice_in_dim(block, block.shape[dim] - width, None, axis...  18.1 us
    dot_general x1, matrix products, body(): localized = jnp.einsum('ij,mjc->mic', localize, direction, precision=hi)  6.79 us
    ppermute x6, waiting for transfers between devices, extended(): lax.ppermute(lax.slice_in_dim(block, 0, width, axis=dim), axis, backward)  4.27 us
  transfers between devices with their start and end apart: 13, of which 12 were waited for; matrix products, arithmetic and copies ran while one was open for 2% of the time, Pallas kernels for 0%

profile of v1, /device:TPU:12, one launch (start us, length us, event | category | flops | bytes accessed | tf_op | source)
XLA Modules:
  0.0 203.5 jit_solution(6216985833287400118)
XLA Ops:
  7.2 6.8 %fusion.6 = f32[2,1024,64]{1,2,0:T(8,128)S(1)} fusion(f32[2,1024,64]{1,2,0:T(8,128)} %param.16, f32[1024,1024]{1,0:T(8,128)} %param.18), kind=kOutput, calls=%fused_computation.10 | convolution fusion | flops 1610612736 | bytes 5242880 | tf_op jit(solution)/shard_map/ij,mjc->mic/dot_general | solution.py:51
  14.1 1.1 fusion.4
  15.3 45.0 %all-gather.3.cloned.1.call-done = f32[12,1024,64]{1,2,0:T(8,128)} async-done(((f32[3,1024,64]{1,2,0:T(8,128)}), f32[12,1024,64]{1,2,0:T(8,128)}) %all-gather.3.cloned.1.call-update) | async-done | bytes 3145744 | tf_op jit(solution)/shard_map/all_gather | solution.py:53
  60.3 2.3 %reduce_sum.65 = f32[3,1024,64]{1,2,0:T(8,128)S(1)} reduce(f32[4,3,1024,64]{2,3,1,0:T(8,128)} %bitcast.22, f32[]{:T(128)} %constant.120.clone.1), dimensions={0}, to_apply=%region_3.4 | reduce | flops 589824 | bytes 3932164 | tf_op jit(solution)/shard_map/reduce_sum | solution.py:53
  63.2 0.9 collective-permute-done
  64.0 1.8 collective-permute-done.1
  68.9 4.2 %collective-permute-done.3 = f32[3,1024,1]{1,2,0:T(1,128)S(1)} collective-permute-done((f32[3,1024,1]{1,2,0:T(1,128)S(1)}, f32[3,1024,1]{1,2,0:T(1,128)S(1)}, u32[]{:S(2)}, u32[]{:S(2)}) %collective-permute-start.3) | collective-permute-done | bytes 12320 | tf_op jit(solution)/shard_map/ppermute | solution.py:17
  73.3 0.9 fusion.82
  74.8 1.3 pad_slice_fusion.7
  76.2 1.1 copy.38
  77.5 1.8 collective-permute-done.5
  79.3 1.1 fusion.57
  80.8 23.0 %gather_fusion = f32[4096]{0:T(1024)S(1)} fusion(f32[196608]{0:T(1024)S(1)} %pad_maximum_fusion.16, s32[4096]{0:T(1024)S(1)} %get-tuple-element.53), kind=kCustom, calls=%fused_computation | custom fusion | bytes 49152 | tf_op jit(solution)/shard_map/gather | solution.py:68
  103.9 22.2 %scatter_custom_fusion = f32[262144]{0:T(1024)S(1)} fusion(s32[4096]{0:T(1024)S(1)} %compare_select_fusion.1, f32[4096]{0:T(1024)S(1)} %multiply_select_fusion, f32[]{:T(128)} %constant.120.clone.1), kind=kCustom, calls=%fused_computation.71 | custom fusion | flops 4096 | bytes 1048580 | tf_op jit(solution)/shard_map/scatter-add | solution.py:70
  126.5 1.3 collective-permute-start.6
  128.3 0.9 collective-permute-done.6
  129.2 2.3 %collective-permute-done.7 = f32[3,1024,1]{1,2,0:T(1,128)S(1)} collective-permute-done((f32[3,1024,1]{1,2,0:T(1,128)S(1)}, f32[3,1024,1]{1,2,0:T(1,128)S(1)}, u32[]{:S(2)}, u32[]{:S(2)}) %collective-permute-start.7) | collective-permute-done | bytes 12320 | tf_op jit(solution)/shard_map/ppermute | solution.py:17
  133.4 1.0 collective-permute-done.8
  134.4 4.2 %collective-permute-done.9 = f32[3,1024,1]{1,2,0:T(1,128)S(1)} collective-permute-done((f32[3,1024,1]{1,2,0:T(1,128)S(1)}, f32[3,1024,1]{1,2,0:T(1,128)S(1)}, u32[]{:S(2)}, u32[]{:S(2)}) %collective-permute-start.9) | collective-permute-done | bytes 12320 | tf_op jit(solution)/shard_map/ppermute | solution.py:17
  140.1 0.9 collective-permute-done.10
  141.0 3.8 %collective-permute-done.11 = f32[3,1024,1]{1,2,0:T(1,128)S(1)} collective-permute-done((f32[3,1024,1]{1,2,0:T(1,128)S(1)}, f32[3,1024,1]{1,2,0:T(1,128)S(1)}, u32[]{:S(2)}, u32[]{:S(2)}) %collective-permute-start.11) | collective-permute-done | bytes 12320 | tf_op jit(solution)/shard_map/ppermute | solution.py:17
  145.8 3.1 %multiply_reduce_fusion = (f32[]{:T(128)}, f32[]{:T(128)}, f32[]{:T(128)}, f32[]{:T(128)}, f32[2,1024,64]{1,2,0:T(8,128)S(1)}) fusion(f32[2,1024,64]{1,2,0:T(8,128)S(1)} %copy-done.3, f32[2,1024,64]{1,2,0:T(8,128)S(1)} %copy-done.1, f32[2,1024,64]{1,2,0:T(8,128)S(1)} %fusion.5, f32[1024,1024]{1,0:T(8,128)S(1)} %copy-done), kind=kOutput, calls=%fused_computation.66 | convolution fusion | flops 1611792384 | bytes 6291472 | tf_op jit(solution)/shard_map/ji,mjc->mic/dot_general | solution.py:77
  148.9 42.5 %all-reduce.7 = (f32[]{:T(128)}, f32[]{:T(128)}, f32[]{:T(128)}, f32[]{:T(128)}) all-reduce(f32[]{:T(128)} %get-tuple-element.41, f32[]{:T(128)} %get-tuple-element.42, f32[]{:T(128)} %get-tuple-element.40, f32[]{:T(128)} %get-tuple-element.39), channel_id=1, replica_groups=mesh['ens'=4,'lon'=8] {'ens','lon'}, use_global_device_ids=true, to_apply=%region_1.0 | all-reduce | flops 4 | bytes 32 | tf_op jit(solution)/shard_map/psum | solution.py:79
  195.4 1.3 multiply_add_fusion
  (77 shorter events, 10.2 us)
Async XLA Ops:
  7.2 6.9 %copy-start.2 = (bf16[2,3,1024,64]{2,3,1,0:T(8,128)(2,1)S(1)}, bf16[2,3,1024,64]{2,3,1,0:T(8,128)(2,1)}, u32[]{:S(2)}) copy-start(bf16[2,3,1024,64]{2,3,1,0:T(8,128)(2,1)} %param.17) | copy-start | bytes 2359300
  7.2 8.1 %copy-start.5 = (s32[4096]{0:T(1024)S(1)}, s32[4096]{0:T(1024)}, u32[]{:S(2)}) copy-start(s32[4096]{0:T(1024)} %param.19) | copy-start | bytes 49156
  7.2 8.1 %copy-start.6 = (s32[4096]{0:T(1024)S(1)}, s32[4096]{0:T(1024)}, u32[]{:S(2)}) copy-start(s32[4096]{0:T(1024)} %param.20) | copy-start | bytes 49156
  7.2 53.1 %all-gather.3.cloned.1.call-start = ((), (), s32[]{:S(2)}) async-start(), calls=%async_computation | async-start | bytes 3932160 | tf_op jit(solution)/shard_map/all_gather | solution.py:53
  62.6 1.5 collective-permute-start
  62.6 3.2 %collective-permute-start.1 = (f32[3,1024,1]{1,2,0:T(1,128)S(1)}, f32[3,1024,1]{1,2,0:T(1,128)S(1)}, u32[]{:S(2)}, u32[]{:S(2)}) collective-permute-start(f32[3,1024,1]{1,2,0:T(1,128)S(1)} %get-tuple-element.95), channel_id=1, source_target_pairs={{0,1},{1,2},{2,3},{3,4},{4,5},{5,6},{6,7},{7,0},{8,9},{9,10},{10,1... | collective-permute-start | bytes 36872 | tf_op jit(solution)/shard_map/ppermute | solution.py:17
  66.7 2.2 %collective-permute-start.2 = (f32[3,1024,1]{1,2,0:T(1,128)S(1)}, f32[3,1024,1]{1,2,0:T(1,128)S(1)}, u32[]{:S(2)}, u32[]{:S(2)}) collective-permute-start(f32[3,1024,1]{1,2,0:T(1,128)S(1)} %get-tuple-element.90), channel_id=1, source_target_pairs={{1,0},{2,1},{3,2},{4,3},{5,4},{6,5},{7,6},{0,7},{9,8},{10,9},{11,1... | collective-permute-start | bytes 36872 | tf_op jit(solution)/shard_map/ppermute | solution.py:20
  67.5 5.6 %collective-permute-start.3 = (f32[3,1024,1]{1,2,0:T(1,128)S(1)}, f32[3,1024,1]{1,2,0:T(1,128)S(1)}, u32[]{:S(2)}, u32[]{:S(2)}) collective-permute-start(f32[3,1024,1]{1,2,0:T(1,128)S(1)} %get-tuple-element.91), channel_id=1, source_target_pairs={{0,1},{1,2},{2,3},{3,4},{4,5},{5,6},{6,7},{7,0},{8,9},{9,10},{10,1... | collective-permute-start | bytes 36872 | tf_op jit(solution)/shard_map/ppermute | solution.py:17
  74.3 3.2 %collective-permute-start.4 = (f32[3,1024,1]{1,2,0:T(1,128)S(1)}, f32[3,1024,1]{1,2,0:T(1,128)S(1)}, u32[]{:S(2)}, u32[]{:S(2)}) collective-permute-start(f32[3,1024,1]{1,2,0:T(1,128)S(1)} %get-tuple-element.85), channel_id=1, source_target_pairs={{1,0},{2,1},{3,2},{4,3},{5,4},{6,5},{7,6},{0,7},{9,8},{10,9},{11,1... | collective-permute-start | bytes 36872 | tf_op jit(solution)/shard_map/ppermute | solution.py:20
  74.3 5.0 %collective-permute-start.5 = (f32[3,1024,1]{1,2,0:T(1,128)S(1)}, f32[3,1024,1]{1,2,0:T(1,128)S(1)}, u32[]{:S(2)}, u32[]{:S(2)}) collective-permute-start(f32[3,1024,1]{1,2,0:T(1,128)S(1)} %get-tuple-element.84), channel_id=1, source_target_pairs={{0,1},{1,2},{2,3},{3,4},{4,5},{5,6},{6,7},{7,0},{8,9},{9,10},{10,1... | collective-permute-start | bytes 36872 | tf_op jit(solution)/shard_map/ppermute | solution.py:17
  80.8 23.1 %copy-start.7 = (f32[4096]{0:T(1024)S(1)}, f32[4096]{0:T(1024)}, u32[]{:S(2)}) copy-start(f32[4096]{0:T(1024)} %param.21) | copy-start | bytes 49156
  126.5 2.7 %collective-permute-start.6 = (f32[3,1024,1]{1,2,0:T(1,128)S(1)}, f32[3,1024,1]{1,2,0:T(1,128)S(1)}, u32[]{:S(2)}, u32[]{:S(2)}) collective-permute-start(f32[3,1024,1]{1,2,0:T(1,128)S(1)} %get-tuple-element.97), channel_id=1, source_target_pairs={{1,0},{2,1},{3,2},{4,3},{5,4},{6,5},{7,6},{0,7},{9,8},{10,9},{11,1... | collective-permute-start | bytes 36872 | tf_op jit(solution)/shard_map/ppermute | solution.py:20
  127.8 3.7 %collective-permute-start.7 = (f32[3,1024,1]{1,2,0:T(1,128)S(1)}, f32[3,1024,1]{1,2,0:T(1,128)S(1)}, u32[]{:S(2)}, u32[]{:S(2)}) collective-permute-start(f32[3,1024,1]{1,2,0:T(1,128)S(1)} %get-tuple-element.98), channel_id=1, source_target_pairs={{0,1},{1,2},{2,3},{3,4},{4,5},{5,6},{6,7},{7,0},{8,9},{9,10},{10,1... | collective-permute-start | bytes 36872 | tf_op jit(solution)/shard_map/ppermute | solution.py:17
  132.4 2.0 %collective-permute-start.8 = (f32[3,1024,1]{1,2,0:T(1,128)S(1)}, f32[3,1024,1]{1,2,0:T(1,128)S(1)}, u32[]{:S(2)}, u32[]{:S(2)}) collective-permute-start(f32[3,1024,1]{1,2,0:T(1,128)S(1)} %get-tuple-element.77), channel_id=1, source_target_pairs={{1,0},{2,1},{3,2},{4,3},{5,4},{6,5},{7,6},{0,7},{9,8},{10,9},{11,1... | collective-permute-start | bytes 36872 | tf_op jit(solution)/shard_map/ppermute | solution.py:20
  133.0 5.6 %collective-permute-start.9 = (f32[3,1024,1]{1,2,0:T(1,128)S(1)}, f32[3,1024,1]{1,2,0:T(1,128)S(1)}, u32[]{:S(2)}, u32[]{:S(2)}) collective-permute-start(f32[3,1024,1]{1,2,0:T(1,128)S(1)} %get-tuple-element.78), channel_id=1, source_target_pairs={{0,1},{1,2},{2,3},{3,4},{4,5},{5,6},{6,7},{7,0},{8,9},{9,10},{10,1... | collective-permute-start | bytes 36872 | tf_op jit(solution)/shard_map/ppermute | solution.py:17
  139.5 1.5 collective-permute-start.10
  139.6 6.2 %copy-start = (f32[1024,1024]{1,0:T(8,128)S(1)}, f32[1024,1024]{1,0:T(8,128)}, u32[]{:S(2)}) copy-start(f32[1024,1024]{1,0:T(8,128)} %param.18) | copy-start | bytes 12582916
  139.6 6.2 %copy-start.1 = (f32[2,1024,64]{1,2,0:T(8,128)S(1)}, f32[2,1024,64]{1,2,0:T(8,128)}, u32[]{:S(2)}) copy-start(f32[2,1024,64]{1,2,0:T(8,128)} %param.16) | copy-start | bytes 1572868
  139.6 6.2 %copy-start.3 = (f32[2,1024,64]{1,2,0:T(8,128)S(1)}, f32[2,1024,64]{1,2,0:T(8,128)}, u32[]{:S(2)}) copy-start(f32[2,1024,64]{1,2,0:T(8,128)} %param.15) | copy-start | bytes 1572868
  139.6 5.1 %collective-permute-start.11 = (f32[3,1024,1]{1,2,0:T(1,128)S(1)}, f32[3,1024,1]{1,2,0:T(1,128)S(1)}, u32[]{:S(2)}, u32[]{:S(2)}) collective-permute-start(f32[3,1024,1]{1,2,0:T(1,128)S(1)} %get-tuple-element.74), channel_id=1, source_target_pairs={{0,1},{1,2},{2,3},{3,4},{4,5},{5,6},{6,7},{7,0},{8,9},{9,10},{10,1... | collective-permute-start | bytes 36872 | tf_op jit(solution)/shard_map/ppermute | solution.py:17
  145.6 49.8 %copy-start.4 = (f32[2,1024,64]{1,2,0:T(8,128)S(1)}, f32[2,1024,64]{1,2,0:T(8,128)}, u32[]{:S(2)}) copy-start(f32[2,1024,64]{1,2,0:T(8,128)} %param.14) | copy-start | bytes 1572868
Sparse Core Ops, SparseCore 0:
  15.3 44.9 all-gather.2
